TPU v7x, 32 devices: a whole 2x2x4 slice. The times are simulated.
32 devices in a mesh: groups: 2 (over x), cube: 16 (over z, y, core).
Axes of the slice: x: 2, y: 2, z: 4, core: 2. Of those that a mesh axis runs over, the one named last changes fastest.
Arguments:
- patches: float32 [1024, 128, 128], P(('groups', 'cube')), parts along dimension 0, may hold values from -6 to 6
- ghost_rows: float32 [1024, 2, 128], P(('groups', 'cube')), parts along dimension 0, may hold values from -6 to 6
- courant: float32 [1024, 2], P(('groups', 'cube')), parts along dimension 0, may hold values from 0.2 to 0.48
- patch_ids: int32 [1024], P(('groups', 'cube')), parts along dimension 0, may hold values from 0 to 511, each once
- initial_load: int32 [32], P(('groups', 'cube')), parts along dimension 0, may hold values from 0 to 32, as said below
- flow_counts: int32 [3, 32, 4], P(None, ('groups', 'cube')), parts along dimension 1, may hold values from 0 to 8, as said below
Outputs:
- advected: float32 [1024, 128, 128], P(('groups', 'cube')), parts along dimension 0
- final_ids: int32 [1024], P(('groups', 'cube')), parts along dimension 0
- imbalance: float32 [6], P('groups'), parts along dimension 0
There are 2 independent parts, one for each index of `groups`. A program takes and returns all parts, laid end to end along the dimension named above; each array names one. Nothing has to cross between parts.
Inputs may be any that keep to these rules, and one draw needn't show every extreme that they name: For some even k drawn from the seed, initial_load[k] = 32 and initial_load[k + 1] = 0. `flow_counts`: of two partners along a dimension at most one sends; a device never sends more than it holds and never holds more than 32. Counts of sweep 0 are at most 8 (reached in every draw), counts of later sweeps at most 4. At no time does a device hold more than 8 records that started on one other device; after the sweeps some device holds exactly 8 records that started on one other device.
All inputs are finite; a program needn't handle non-finite values.
Results may differ from a plain program's by a relative error of at most 0.0003.
Values sent between devices are 32-bit elements; how exact they have to be, the bound alone decides.
A program may use at most 64 MiB of HBM per device.

v0:
```python
import jax
import jax.numpy as jnp
from jax import lax
from jax.sharding import PartitionSpec as P

SWEEPS = 3


def swapped(value, axis, bit):
    mask = 2**bit
    pairs = [(source, source ^ mask) for source in range(lax.axis_size(axis))]
    return lax.ppermute(value, axis, pairs)


def cut_rows(source, first_free, capacity):
    padded = jnp.concatenate([source, jnp.zeros((capacity,) + source.shape[1:], source.dtype)], 0)
    return lax.dynamic_slice_in_dim(padded, first_free, capacity, 0)


def place_rows(source, spare_rows, first_free, incoming, capacity):
    slot_count = source.shape[0]
    shape_tail = (1,) * (source.ndim - 1)
    row_index = jnp.arange(slot_count, dtype=jnp.int32).reshape((slot_count,) + shape_tail)
    retained = jnp.where(row_index < first_free, source, jnp.zeros_like(source))
    extra_index = jnp.arange(capacity, dtype=jnp.int32).reshape((capacity,) + shape_tail)
    landed = jnp.where(extra_index < incoming, spare_rows, jnp.zeros_like(spare_rows))
    padded = jnp.concatenate([retained, jnp.zeros((capacity,) + source.shape[1:], source.dtype)], 0)
    return lax.dynamic_update_slice_in_dim(padded, landed, first_free, 0)[:slot_count]


def advect(field, ghost_rows, courant, holding):
    western = jnp.concatenate([ghost_rows[:, 1, :][:, :, None], field[:, :, :-1]], 2)
    northern = jnp.concatenate([ghost_rows[:, 0, :][:, None, :], field[:, :-1, :]], 1)
    along_x = courant[:, 0][:, None, None]
    along_y = courant[:, 1][:, None, None]
    stepped = field - along_x * (field - western) - along_y * (field - northern)
    row_index = jnp.arange(field.shape[0], dtype=jnp.int32)[:, None, None]
    return jnp.where(row_index < holding, stepped, jnp.zeros_like(stepped))


def migrate(resident, holding, outgoing, capacity, dim_no):
    first_free = holding - outgoing
    outbox = [cut_rows(source, first_free, capacity) for source in resident]
    arrived = swapped(
        (outbox[0], outbox[1], outbox[2], outbox[3], outgoing.reshape(1)), "cube", dim_no
    )
    incoming = arrived[4][0]
    placed = [
        place_rows(source, arrived[slot_no], first_free, incoming, capacity)
        for slot_no, source in enumerate(resident)
    ]
    return (placed, first_free + incoming)


def shards(patches, ghost_rows, courant, patch_ids, initial_load, flow_counts):
    cube_size = lax.axis_size("cube")
    dim_total = cube_size.bit_length() - 1
    slot_count = patches.shape[0]
    resident = [patches, ghost_rows, courant, patch_ids]
    holding = initial_load[0]
    total_load = lax.psum(jnp.sum(initial_load.astype(jnp.float32)), "cube")
    peak_loads = []
    for sweep_no in range(SWEEPS):
        capacity = slot_count // 4 if sweep_no == 0 else slot_count // 8
        for dim_no in range(dim_total):
            resident, holding = migrate(
                resident, holding, flow_counts[sweep_no, 0, dim_no], capacity, dim_no
            )
        peak_loads.append(lax.pmax(holding.astype(jnp.float32), "cube"))
    stacked = jnp.stack(peak_loads)
    imbalance = stacked * float(cube_size) / total_load
    advected = advect(resident[0], resident[1], resident[2], holding)
    row_index = jnp.arange(slot_count, dtype=jnp.int32)
    final_ids = jnp.where(row_index < holding, resident[3], -1)
    return (advected, final_ids, imbalance)


def solution(mesh):
    in_specs = (
        P(("groups", "cube"), None, None),
        P(("groups", "cube"), None, None),
        P(("groups", "cube"), None),
        P(("groups", "cube")),
        P(("groups", "cube")),
        P(None, ("groups", "cube"), None),
    )
    out_specs = (P(("groups", "cube"), None, None), P(("groups", "cube")), P("groups"))
    return jax.shard_map(shards, mesh=mesh, in_specs=in_specs, out_specs=out_specs, check_vma=False)
```

profile of v0, /device:TPU:0, one launch (start us, length us, event | category | flops | bytes accessed | tf_op | source)
XLA Modules:
  0.0 349.9 jit_solution(7194449375796047109)
XLA Ops:
  4.9 3.6 %collective-permute-start.11 = (s32[1]{0:T(128)}, s32[1]{0:T(128)}, u32[]{:S(2)}, u32[]{:S(2)}) collective-permute-start(s32[1]{0:T(128)} %bitcast.35), channel_id=1, source_target_pairs={{0,8},{1,9},{2,10},{3,11},{4,12},{5,13},{6,14},{7,15},{8,0},{9,1},... | collective-permute-start | bytes 20 | tf_op jit(solution)/shard_map/ppermute | solution.py:12
  16.0 31.5 %psum.7 = f32[]{:T(128)} all-reduce(f32[]{:T(128)} %bitcast.44), channel_id=1, replica_groups=mesh['groups'=2,'cube'=16] {'cube'}, use_global_device_ids=true, to_apply=%region_3.4 | all-reduce | flops 1 | bytes 8 | tf_op jit(solution)/shard_map/psum | solution.py:61
  50.9 2.5 collective-permute-done.1
  59.0 2.6 collective-permute-done.3
  73.1 2.3 collective-permute-done.7
  86.1 33.7 %all-reduce.52 = (f32[1]{0:T(128)}, f32[1]{0:T(128)}, f32[1]{0:T(128)}) all-reduce(f32[1]{0:T(128)} %bitcast.43, f32[1]{0:T(128)} %bitcast.42, f32[1]{0:T(128)} %bitcast.41), channel_id=1, replica_groups=mesh['groups'=2,'cube'=16] {'cube'}, use_global_device_ids=true, to_apply=%region_2.3 | all-reduce | flops 3 | bytes 24 | tf_op jit(solution)/shard_map/pmax | solution.py:69
  119.9 3.1 fusion.16
  124.0 3.6 %collective-permute-done.49 = s32[8]{0:T(128)S(1)} collective-permute-done((s32[8]{0:T(128)S(1)}, s32[8]{0:T(128)S(1)}, u32[]{:S(2)}, u32[]{:S(2)}) %collective-permute-start.49) | collective-permute-done | bytes 64 | tf_op jit(solution)/shard_map/ppermute | solution.py:12
  128.8 3.2 collective-permute-done.50
  132.8 4.5 %collective-permute-done.51 = s32[8]{0:T(128)S(1)} collective-permute-done((s32[8]{0:T(128)S(1)}, s32[8]{0:T(128)S(1)}, u32[]{:S(2)}, u32[]{:S(2)}) %collective-permute-start.51) | collective-permute-done | bytes 64 | tf_op jit(solution)/shard_map/ppermute | solution.py:12
  140.2 3.5 collective-permute-done.53
  145.8 2.3 collective-permute-done.54
  149.0 4.5 %collective-permute-done.55 = s32[4]{0:T(128)S(1)} collective-permute-done((s32[4]{0:T(128)S(1)}, s32[4]{0:T(128)S(1)}, u32[]{:S(2)}, u32[]{:S(2)}) %collective-permute-start.55) | collective-permute-done | bytes 48 | tf_op jit(solution)/shard_map/ppermute | solution.py:12
  156.3 3.5 collective-permute-done.57
  161.8 2.3 collective-permute-done.58
  164.9 2.2 collective-permute-start.59
  167.1 2.3 collective-permute-done.59
  172.6 3.5 collective-permute-done.29
  177.7 2.3 collective-permute-done.30
  180.3 2.2 collective-permute-start.31
  182.5 2.3 collective-permute-done.31
  186.7 3.5 collective-permute-done.33
  191.7 2.3 collective-permute-done.34
  194.4 2.2 collective-permute-start.35
  196.5 2.3 collective-permute-done.35
  199.4 3.5 collective-permute-done.37
  204.5 2.3 collective-permute-done.38
  207.0 2.2 collective-permute-start.39
  209.3 2.3 collective-permute-done.39
  213.4 3.4 collective-permute-done.41
  218.4 2.3 collective-permute-done.42
  220.9 2.2 collective-permute-start.43
  223.1 2.3 collective-permute-done.43
  227.2 3.4 collective-permute-done.45
  232.2 2.3 collective-permute-done.46
  235.1 2.2 collective-permute-start.47
  237.8 8.9 %collective-permute-done.13 = f32[8,128,128]{2,1,0:T(8,128)S(1)} collective-permute-done((f32[8,128,128]{2,1,0:T(8,128)S(1)}, f32[8,128,128]{2,1,0:T(8,128)S(1)}, u32[]{:S(2)}, u32[]{:S(2)}) %collective-permute-start.13) | collective-permute-done | bytes 524320 | tf_op jit(solution)/shard_map/ppermute | solution.py:12
  249.8 8.9 %collective-permute-done.14 = f32[8,128,128]{2,1,0:T(8,128)S(1)} collective-permute-done((f32[8,128,128]{2,1,0:T(8,128)}, f32[8,128,128]{2,1,0:T(8,128)S(1)}, u32[]{:S(2)}, u32[]{:S(2)}) %collective-permute-start.14) | collective-permute-done | bytes 524320 | tf_op jit(solution)/shard_map/ppermute | solution.py:12
  259.8 2.2 collective-permute-start.15
  261.9 2.0 copy.14
  264.4 17.7 %collective-permute-done.15 = f32[8,128,128]{2,1,0:T(8,128)S(1)} collective-permute-done((f32[8,128,128]{2,1,0:T(8,128)}, f32[8,128,128]{2,1,0:T(8,128)S(1)}, u32[]{:S(2)}, u32[]{:S(2)}) %collective-permute-start.15) | collective-permute-done | bytes 524320 | tf_op jit(solution)/shard_map/ppermute | solution.py:12
  285.5 7.2 %collective-permute-done.17 = f32[4,128,128]{2,1,0:T(8,128)S(1)} collective-permute-done((f32[4,128,128]{2,1,0:T(8,128)S(1)}, f32[4,128,128]{2,1,0:T(8,128)S(1)}, u32[]{:S(2)}, u32[]{:S(2)}) %collective-permute-start.17) | collective-permute-done | bytes 262176 | tf_op jit(solution)/shard_map/ppermute | solution.py:12
  293.5 6.9 %collective-permute-done.18 = f32[4,128,128]{2,1,0:T(8,128)S(1)} collective-permute-done((f32[4,128,128]{2,1,0:T(8,128)S(1)}, f32[4,128,128]{2,1,0:T(8,128)S(1)}, u32[]{:S(2)}, u32[]{:S(2)}) %collective-permute-start.18) | collective-permute-done | bytes 262176 | tf_op jit(solution)/shard_map/ppermute | solution.py:12
  302.8 11.0 %collective-permute-done.19 = f32[4,128,128]{2,1,0:T(8,128)S(1)} collective-permute-done((f32[4,128,128]{2,1,0:T(8,128)S(1)}, f32[4,128,128]{2,1,0:T(8,128)S(1)}, u32[]{:S(2)}, u32[]{:S(2)}) %collective-permute-start.19) | collective-permute-done | bytes 262176 | tf_op jit(solution)/shard_map/ppermute | solution.py:12
  317.0 7.2 %collective-permute-done.21 = f32[4,128,128]{2,1,0:T(8,128)S(1)} collective-permute-done((f32[4,128,128]{2,1,0:T(8,128)S(1)}, f32[4,128,128]{2,1,0:T(8,128)S(1)}, u32[]{:S(2)}, u32[]{:S(2)}) %collective-permute-start.21) | collective-permute-done | bytes 262176 | tf_op jit(solution)/shard_map/ppermute | solution.py:12
  325.0 7.0 %collective-permute-done.22 = f32[4,128,128]{2,1,0:T(8,128)S(1)} collective-permute-done((f32[4,128,128]{2,1,0:T(8,128)S(1)}, f32[4,128,128]{2,1,0:T(8,128)S(1)}, u32[]{:S(2)}, u32[]{:S(2)}) %collective-permute-start.22) | collective-permute-done | bytes 262176 | tf_op jit(solution)/shard_map/ppermute | solution.py:12
  334.3 11.0 %collective-permute-done.23 = f32[4,128,128]{2,1,0:T(8,128)S(1)} collective-permute-done((f32[4,128,128]{2,1,0:T(8,128)S(1)}, f32[4,128,128]{2,1,0:T(8,128)S(1)}, u32[]{:S(2)}, u32[]{:S(2)}) %collective-permute-start.23) | collective-permute-done | bytes 262176 | tf_op jit(solution)/shard_map/ppermute | solution.py:12
  347.2 2.7 fusion.3
  (359 shorter events, 79.6 us)
Async XLA Ops:
  4.4 118.7 %collective-permute-start.48 = (s32[8]{0:T(128)S(1)}, s32[8]{0:T(128)S(1)}, u32[]{:S(2)}, u32[]{:S(2)}) collective-permute-start(s32[8]{0:T(128)S(1)} %pad_dynamic-slice_fusion.2), channel_id=1, source_target_pairs={{0,1},{1,0},{2,3},{3,2},{4,5},{5,4},{6,7},{7,6},{8,9},{9,8},{10,11... | collective-permute-start | bytes 104 | tf_op jit(solution)/shard_map/ppermute | solution.py:12
  4.9 79.2 %collective-permute-start.11 = (s32[1]{0:T(128)}, s32[1]{0:T(128)}, u32[]{:S(2)}, u32[]{:S(2)}) collective-permute-start(s32[1]{0:T(128)} %bitcast.35), channel_id=1, source_target_pairs={{0,8},{1,9},{2,10},{3,11},{4,12},{5,13},{6,14},{7,15},{8,0},{9,1},... | collective-permute-start | bytes 20 | tf_op jit(solution)/shard_map/ppermute | solution.py:12
  8.5 71.2 %collective-permute-start.9 = (s32[1]{0:T(128)}, s32[1]{0:T(128)}, u32[]{:S(2)}, u32[]{:S(2)}) collective-permute-start(s32[1]{0:T(128)} %bitcast.29), channel_id=1, source_target_pairs={{0,2},{1,3},{2,0},{3,1},{4,6},{5,7},{6,4},{7,5},{8,10},{9,11},{10,... | collective-permute-start | bytes 20 | tf_op jit(solution)/shard_map/ppermute | solution.py:12
  10.0 67.5 %collective-permute-start.8 = (s32[1]{0:T(128)}, s32[1]{0:T(128)}, u32[]{:S(2)}, u32[]{:S(2)}) collective-permute-start(s32[1]{0:T(128)} %bitcast.26), channel_id=1, source_target_pairs={{0,1},{1,0},{2,3},{3,2},{4,5},{5,4},{6,7},{7,6},{8,9},{9,8},{10,11... | collective-permute-start | bytes 20 | tf_op jit(solution)/shard_map/ppermute | solution.py:12
  10.0 39.6 %collective-permute-start = (s32[1]{0:T(128)}, s32[1]{0:T(128)}, u32[]{:S(2)}, u32[]{:S(2)}) collective-permute-start(s32[1]{0:T(128)} %bitcast.2), channel_id=1, source_target_pairs={{0,1},{1,0},{2,3},{3,2},{4,5},{5,4},{6,7},{7,6},{8,9},{9,8},{10,11... | collective-permute-start | bytes 20 | tf_op jit(solution)/shard_map/ppermute | solution.py:12
  49.6 3.8 %collective-permute-start.1 = (s32[1]{0:T(128)}, s32[1]{0:T(128)}, u32[]{:S(2)}, u32[]{:S(2)}) collective-permute-start(s32[1]{0:T(128)} %bitcast.5), channel_id=1, source_target_pairs={{0,2},{1,3},{2,0},{3,1},{4,6},{5,7},{6,4},{7,5},{8,10},{9,11},{10,... | collective-permute-start | bytes 20 | tf_op jit(solution)/shard_map/ppermute | solution.py:12
  53.4 3.7 %collective-permute-start.2 = (s32[1]{0:T(128)}, s32[1]{0:T(128)}, u32[]{:S(2)}, u32[]{:S(2)}) collective-permute-start(s32[1]{0:T(128)} %bitcast.8), channel_id=1, source_target_pairs={{0,4},{1,5},{2,6},{3,7},{4,0},{5,1},{6,2},{7,3},{8,12},{9,13},{10,... | collective-permute-start | bytes 20 | tf_op jit(solution)/shard_map/ppermute | solution.py:12
  57.2 4.5 %collective-permute-start.3 = (s32[1]{0:T(128)}, s32[1]{0:T(128)}, u32[]{:S(2)}, u32[]{:S(2)}) collective-permute-start(s32[1]{0:T(128)} %bitcast.11), channel_id=1, source_target_pairs={{0,8},{1,9},{2,10},{3,11},{4,12},{5,13},{6,14},{7,15},{8,0},{9,1},... | collective-permute-start | bytes 20 | tf_op jit(solution)/shard_map/ppermute | solution.py:12
  63.0 3.8 %collective-permute-start.5 = (s32[1]{0:T(128)}, s32[1]{0:T(128)}, u32[]{:S(2)}, u32[]{:S(2)}) collective-permute-start(s32[1]{0:T(128)} %bitcast.17), channel_id=1, source_target_pairs={{0,2},{1,3},{2,0},{3,1},{4,6},{5,7},{6,4},{7,5},{8,10},{9,11},{10,... | collective-permute-start | bytes 20 | tf_op jit(solution)/shard_map/ppermute | solution.py:12
  66.8 3.9 %collective-permute-start.6 = (s32[1]{0:T(128)}, s32[1]{0:T(128)}, u32[]{:S(2)}, u32[]{:S(2)}) collective-permute-start(s32[1]{0:T(128)} %bitcast.20), channel_id=1, source_target_pairs={{0,4},{1,5},{2,6},{3,7},{4,0},{5,1},{6,2},{7,3},{8,12},{9,13},{10,... | collective-permute-start | bytes 20 | tf_op jit(solution)/shard_map/ppermute | solution.py:12
  70.7 4.6 %collective-permute-start.7 = (s32[1]{0:T(128)}, s32[1]{0:T(128)}, u32[]{:S(2)}, u32[]{:S(2)}) collective-permute-start(s32[1]{0:T(128)} %bitcast.23), channel_id=1, source_target_pairs={{0,8},{1,9},{2,10},{3,11},{4,12},{5,13},{6,14},{7,15},{8,0},{9,1},... | collective-permute-start | bytes 20 | tf_op jit(solution)/shard_map/ppermute | solution.py:12
  75.3 7.4 %collective-permute-start.10 = (s32[1]{0:T(128)}, s32[1]{0:T(128)}, u32[]{:S(2)}, u32[]{:S(2)}) collective-permute-start(s32[1]{0:T(128)} %bitcast.32), channel_id=1, source_target_pairs={{0,4},{1,5},{2,6},{3,7},{4,0},{5,1},{6,2},{7,3},{8,12},{9,13},{10,... | collective-permute-start | bytes 20 | tf_op jit(solution)/shard_map/ppermute | solution.py:12
  77.6 50.9 %collective-permute-start.24 = (f32[8,2]{0,1:T(2,128)S(1)}, f32[8,2]{0,1:T(2,128)S(1)}, u32[]{:S(2)}, u32[]{:S(2)}) collective-permute-start(f32[8,2]{0,1:T(2,128)S(1)} %constant_dynamic-slice_fusion.22), channel_id=1, source_target_pairs={{0,1},{1,0},{2,3},{3,2},{4,5},{5,4},{6,7},{7,6},{8,9},{9,8},{10,11... | collective-permute-start | bytes 200 | tf_op jit(solution)/shard_map/ppermute | solution.py:12
  79.7 119.4 %collective-permute-start.36 = (f32[8,2,128]{2,0,1:T(8,128)S(1)}, f32[8,2,128]{2,0,1:T(8,128)S(1)}, u32[]{:S(2)}, u32[]{:S(2)}) collective-permute-start(f32[8,2,128]{2,0,1:T(8,128)S(1)} %pad_dynamic-slice_fusion.1), channel_id=1, source_target_pairs={{0,1},{1,0},{2,3},{3,2},{4,5},{5,4},{6,7},{7,6},{8,9},{9,8},{10,11... | collective-permute-start | bytes 24584 | tf_op jit(solution)/shard_map/ppermute | solution.py:12
  82.8 151.9 %collective-permute-start.12 = (f32[8,128,128]{2,1,0:T(8,128)}, f32[8,128,128]{2,1,0:T(8,128)S(1)}, u32[]{:S(2)}, u32[]{:S(2)}) collective-permute-start(f32[8,128,128]{2,1,0:T(8,128)} %pad_dynamic-slice_fusion), channel_id=1, source_target_pairs={{0,1},{1,0},{2,3},{3,2},{4,5},{5,4},{6,7},{7,6},{8,9},{9,8},{10,11... | collective-permute-start | bytes 1572872 | tf_op jit(solution)/shard_map/ppermute | solution.py:12
  123.9 3.6 %collective-permute-start.49 = (s32[8]{0:T(128)S(1)}, s32[8]{0:T(128)S(1)}, u32[]{:S(2)}, u32[]{:S(2)}) collective-permute-start(s32[8]{0:T(128)S(1)} %dynamic_slice.181), channel_id=1, source_target_pairs={{0,2},{1,3},{2,0},{3,1},{4,6},{5,7},{6,4},{7,5},{8,10},{9,11},{10,... | collective-permute-start | bytes 104 | tf_op jit(solution)/shard_map/ppermute | solution.py:12
  128.4 3.6 %collective-permute-start.50 = (s32[8]{0:T(128)S(1)}, s32[8]{0:T(128)S(1)}, u32[]{:S(2)}, u32[]{:S(2)}) collective-permute-start(s32[8]{0:T(128)S(1)} %dynamic_slice.182), channel_id=1, source_target_pairs={{0,4},{1,5},{2,6},{3,7},{4,0},{5,1},{6,2},{7,3},{8,12},{9,13},{10,... | collective-permute-start | bytes 104 | tf_op jit(solution)/shard_map/ppermute | solution.py:12
  128.8 9.3 %collective-permute-start.25 = (f32[8,2]{0,1:T(2,128)S(1)}, f32[8,2]{0,1:T(2,128)S(1)}, u32[]{:S(2)}, u32[]{:S(2)}) collective-permute-start(f32[8,2]{0,1:T(2,128)S(1)} %constant_dynamic-slice_fusion.21), channel_id=1, source_target_pairs={{0,2},{1,3},{2,0},{3,1},{4,6},{5,7},{6,4},{7,5},{8,10},{9,11},{10,... | collective-permute-start | bytes 200 | tf_op jit(solution)/shard_map/ppermute | solution.py:12
  132.7 4.5 %collective-permute-start.51 = (s32[8]{0:T(128)S(1)}, s32[8]{0:T(128)S(1)}, u32[]{:S(2)}, u32[]{:S(2)}) collective-permute-start(s32[8]{0:T(128)S(1)} %dynamic_slice.183), channel_id=1, source_target_pairs={{0,8},{1,9},{2,10},{3,11},{4,12},{5,13},{6,14},{7,15},{8,0},{9,1},... | collective-permute-start | bytes 104 | tf_op jit(solution)/shard_map/ppermute | solution.py:12
  138.5 15.7 %collective-permute-start.26 = (f32[8,2]{0,1:T(2,128)S(1)}, f32[8,2]{0,1:T(2,128)S(1)}, u32[]{:S(2)}, u32[]{:S(2)}) collective-permute-start(f32[8,2]{0,1:T(2,128)S(1)} %constant_dynamic-slice_fusion.20), channel_id=1, source_target_pairs={{0,4},{1,5},{2,6},{3,7},{4,0},{5,1},{6,2},{7,3},{8,12},{9,13},{10,... | collective-permute-start | bytes 200 | tf_op jit(solution)/shard_map/ppermute | solution.py:12
  140.1 3.6 %collective-permute-start.53 = (s32[4]{0:T(128)S(1)}, s32[4]{0:T(128)S(1)}, u32[]{:S(2)}, u32[]{:S(2)}) collective-permute-start(s32[4]{0:T(128)S(1)} %dynamic_slice.185), channel_id=1, source_target_pairs={{0,2},{1,3},{2,0},{3,1},{4,6},{5,7},{6,4},{7,5},{8,10},{9,11},{10,... | collective-permute-start | bytes 56 | tf_op jit(solution)/shard_map/ppermute | solution.py:12
  148.9 4.5 %collective-permute-start.55 = (s32[4]{0:T(128)S(1)}, s32[4]{0:T(128)S(1)}, u32[]{:S(2)}, u32[]{:S(2)}) collective-permute-start(s32[4]{0:T(128)S(1)} %dynamic_slice.187), channel_id=1, source_target_pairs={{0,8},{1,9},{2,10},{3,11},{4,12},{5,13},{6,14},{7,15},{8,0},{9,1},... | collective-permute-start | bytes 56 | tf_op jit(solution)/shard_map/ppermute | solution.py:12
  154.6 16.2 %collective-permute-start.27 = (f32[8,2]{0,1:T(2,128)S(1)}, f32[8,2]{0,1:T(2,128)S(1)}, u32[]{:S(2)}, u32[]{:S(2)}) collective-permute-start(f32[8,2]{0,1:T(2,128)S(1)} %constant_dynamic-slice_fusion.19), channel_id=1, source_target_pairs={{0,8},{1,9},{2,10},{3,11},{4,12},{5,13},{6,14},{7,15},{8,0},{9,1},... | collective-permute-start | bytes 200 | tf_op jit(solution)/shard_map/ppermute | solution.py:12
  164.9 4.5 %collective-permute-start.59 = (s32[4]{0:T(128)S(1)}, s32[4]{0:T(128)S(1)}, u32[]{:S(2)}, u32[]{:S(2)}) collective-permute-start(s32[4]{0:T(128)S(1)} %dynamic_slice.191), channel_id=1, source_target_pairs={{0,8},{1,9},{2,10},{3,11},{4,12},{5,13},{6,14},{7,15},{8,0},{9,1},... | collective-permute-start | bytes 56 | tf_op jit(solution)/shard_map/ppermute | solution.py:12
  172.6 3.6 %collective-permute-start.29 = (f32[4,2]{0,1:T(2,128)S(1)}, f32[4,2]{0,1:T(2,128)S(1)}, u32[]{:S(2)}, u32[]{:S(2)}) collective-permute-start(f32[4,2]{0,1:T(2,128)S(1)} %constant_dynamic-slice_fusion.17), channel_id=1, source_target_pairs={{0,2},{1,3},{2,0},{3,1},{4,6},{5,7},{6,4},{7,5},{8,10},{9,11},{10,... | collective-permute-start | bytes 104 | tf_op jit(solution)/shard_map/ppermute | solution.py:12
  176.4 3.6 %collective-permute-start.30 = (f32[4,2]{0,1:T(2,128)S(1)}, f32[4,2]{0,1:T(2,128)S(1)}, u32[]{:S(2)}, u32[]{:S(2)}) collective-permute-start(f32[4,2]{0,1:T(2,128)S(1)} %constant_dynamic-slice_fusion.16), channel_id=1, source_target_pairs={{0,4},{1,5},{2,6},{3,7},{4,0},{5,1},{6,2},{7,3},{8,12},{9,13},{10,... | collective-permute-start | bytes 104 | tf_op jit(solution)/shard_map/ppermute | solution.py:12
  180.3 4.5 %collective-permute-start.31 = (f32[4,2]{0,1:T(2,128)S(1)}, f32[4,2]{0,1:T(2,128)S(1)}, u32[]{:S(2)}, u32[]{:S(2)}) collective-permute-start(f32[4,2]{0,1:T(2,128)S(1)} %constant_dynamic-slice_fusion.15), channel_id=1, source_target_pairs={{0,8},{1,9},{2,10},{3,11},{4,12},{5,13},{6,14},{7,15},{8,0},{9,1},... | collective-permute-start | bytes 104 | tf_op jit(solution)/shard_map/ppermute | solution.py:12
  186.6 3.6 %collective-permute-start.33 = (f32[4,2]{0,1:T(2,128)S(1)}, f32[4,2]{0,1:T(2,128)S(1)}, u32[]{:S(2)}, u32[]{:S(2)}) collective-permute-start(f32[4,2]{0,1:T(2,128)S(1)} %constant_dynamic-slice_fusion.13), channel_id=1, source_target_pairs={{0,2},{1,3},{2,0},{3,1},{4,6},{5,7},{6,4},{7,5},{8,10},{9,11},{10,... | collective-permute-start | bytes 104 | tf_op jit(solution)/shard_map/ppermute | solution.py:12
  190.5 3.6 %collective-permute-start.34 = (f32[4,2]{0,1:T(2,128)S(1)}, f32[4,2]{0,1:T(2,128)S(1)}, u32[]{:S(2)}, u32[]{:S(2)}) collective-permute-start(f32[4,2]{0,1:T(2,128)S(1)} %constant_dynamic-slice_fusion.12), channel_id=1, source_target_pairs={{0,4},{1,5},{2,6},{3,7},{4,0},{5,1},{6,2},{7,3},{8,12},{9,13},{10,... | collective-permute-start | bytes 104 | tf_op jit(solution)/shard_map/ppermute | solution.py:12
  194.4 4.5 %collective-permute-start.35 = (f32[4,2]{0,1:T(2,128)S(1)}, f32[4,2]{0,1:T(2,128)S(1)}, u32[]{:S(2)}, u32[]{:S(2)}) collective-permute-start(f32[4,2]{0,1:T(2,128)S(1)} %constant_dynamic-slice_fusion.11), channel_id=1, source_target_pairs={{0,8},{1,9},{2,10},{3,11},{4,12},{5,13},{6,14},{7,15},{8,0},{9,1},... | collective-permute-start | bytes 104 | tf_op jit(solution)/shard_map/ppermute | solution.py:12
  199.3 3.7 %collective-permute-start.37 = (f32[8,2,128]{2,0,1:T(8,128)S(1)}, f32[8,2,128]{2,0,1:T(8,128)S(1)}, u32[]{:S(2)}, u32[]{:S(2)}) collective-permute-start(f32[8,2,128]{2,0,1:T(8,128)S(1)} %fusion.5), channel_id=1, source_target_pairs={{0,2},{1,3},{2,0},{3,1},{4,6},{5,7},{6,4},{7,5},{8,10},{9,11},{10,... | collective-permute-start | bytes 24584 | tf_op jit(solution)/shard_map/ppermute | solution.py:12
  203.1 3.7 %collective-permute-start.38 = (f32[8,2,128]{2,0,1:T(8,128)S(1)}, f32[8,2,128]{2,0,1:T(8,128)S(1)}, u32[]{:S(2)}, u32[]{:S(2)}) collective-permute-start(f32[8,2,128]{2,0,1:T(8,128)S(1)} %fusion.6), channel_id=1, source_target_pairs={{0,4},{1,5},{2,6},{3,7},{4,0},{5,1},{6,2},{7,3},{8,12},{9,13},{10,... | collective-permute-start | bytes 24584 | tf_op jit(solution)/shard_map/ppermute | solution.py:12
  207.0 4.6 %collective-permute-start.39 = (f32[8,2,128]{2,0,1:T(8,128)S(1)}, f32[8,2,128]{2,0,1:T(8,128)S(1)}, u32[]{:S(2)}, u32[]{:S(2)}) collective-permute-start(f32[8,2,128]{2,0,1:T(8,128)S(1)} %fusion.7), channel_id=1, source_target_pairs={{0,8},{1,9},{2,10},{3,11},{4,12},{5,13},{6,14},{7,15},{8,0},{9,1},... | collective-permute-start | bytes 24584 | tf_op jit(solution)/shard_map/ppermute | solution.py:12
  213.2 3.6 %collective-permute-start.41 = (f32[4,2,128]{2,0,1:T(4,128)S(1)}, f32[4,2,128]{2,0,1:T(4,128)S(1)}, u32[]{:S(2)}, u32[]{:S(2)}) collective-permute-start(f32[4,2,128]{2,0,1:T(4,128)S(1)} %fusion.9), channel_id=1, source_target_pairs={{0,2},{1,3},{2,0},{3,1},{4,6},{5,7},{6,4},{7,5},{8,10},{9,11},{10,... | collective-permute-start | bytes 12296 | tf_op jit(solution)/shard_map/ppermute | solution.py:12
  217.0 3.6 %collective-permute-start.42 = (f32[4,2,128]{2,0,1:T(4,128)S(1)}, f32[4,2,128]{2,0,1:T(4,128)S(1)}, u32[]{:S(2)}, u32[]{:S(2)}) collective-permute-start(f32[4,2,128]{2,0,1:T(4,128)S(1)} %fusion.10), channel_id=1, source_target_pairs={{0,4},{1,5},{2,6},{3,7},{4,0},{5,1},{6,2},{7,3},{8,12},{9,13},{10,... | collective-permute-start | bytes 12296 | tf_op jit(solution)/shard_map/ppermute | solution.py:12
  220.9 4.5 %collective-permute-start.43 = (f32[4,2,128]{2,0,1:T(4,128)S(1)}, f32[4,2,128]{2,0,1:T(4,128)S(1)}, u32[]{:S(2)}, u32[]{:S(2)}) collective-permute-start(f32[4,2,128]{2,0,1:T(4,128)S(1)} %fusion.11), channel_id=1, source_target_pairs={{0,8},{1,9},{2,10},{3,11},{4,12},{5,13},{6,14},{7,15},{8,0},{9,1},... | collective-permute-start | bytes 12296 | tf_op jit(solution)/shard_map/ppermute | solution.py:12
  227.0 3.6 %collective-permute-start.45 = (f32[4,2,128]{2,0,1:T(4,128)S(1)}, f32[4,2,128]{2,0,1:T(4,128)S(1)}, u32[]{:S(2)}, u32[]{:S(2)}) collective-permute-start(f32[4,2,128]{2,0,1:T(4,128)S(1)} %fusion.13), channel_id=1, source_target_pairs={{0,2},{1,3},{2,0},{3,1},{4,6},{5,7},{6,4},{7,5},{8,10},{9,11},{10,... | collective-permute-start | bytes 12296 | tf_op jit(solution)/shard_map/ppermute | solution.py:12
  230.8 3.6 %collective-permute-start.46 = (f32[4,2,128]{2,0,1:T(4,128)S(1)}, f32[4,2,128]{2,0,1:T(4,128)S(1)}, u32[]{:S(2)}, u32[]{:S(2)}) collective-permute-start(f32[4,2,128]{2,0,1:T(4,128)S(1)} %fusion.14), channel_id=1, source_target_pairs={{0,4},{1,5},{2,6},{3,7},{4,0},{5,1},{6,2},{7,3},{8,12},{9,13},{10,... | collective-permute-start | bytes 12296 | tf_op jit(solution)/shard_map/ppermute | solution.py:12
  234.9 11.8 %collective-permute-start.13 = (f32[8,128,128]{2,1,0:T(8,128)S(1)}, f32[8,128,128]{2,1,0:T(8,128)S(1)}, u32[]{:S(2)}, u32[]{:S(2)}) collective-permute-start(f32[8,128,128]{2,1,0:T(8,128)S(1)} %dynamic-slice_select_fusion.2), channel_id=1, source_target_pairs={{0,2},{1,3},{2,0},{3,1},{4,6},{5,7},{6,4},{7,5},{8,10},{9,11},{10,... | collective-permute-start | bytes 1572872 | tf_op jit(solution)/shard_map/ppermute | solution.py:12
  235.1 13.8 %collective-permute-start.47 = (f32[4,2,128]{2,0,1:T(4,128)S(1)}, f32[4,2,128]{2,0,1:T(4,128)S(1)}, u32[]{:S(2)}, u32[]{:S(2)}) collective-permute-start(f32[4,2,128]{2,0,1:T(4,128)S(1)} %fusion.15), channel_id=1, source_target_pairs={{0,8},{1,9},{2,10},{3,11},{4,12},{5,13},{6,14},{7,15},{8,0},{9,1},... | collective-permute-start | bytes 12296 | tf_op jit(solution)/shard_map/ppermute | solution.py:12
  247.7 11.0 %collective-permute-start.14 = (f32[8,128,128]{2,1,0:T(8,128)}, f32[8,128,128]{2,1,0:T(8,128)S(1)}, u32[]{:S(2)}, u32[]{:S(2)}) collective-permute-start(f32[8,128,128]{2,1,0:T(8,128)} %dynamic-slice_select_fusion.1), channel_id=1, source_target_pairs={{0,4},{1,5},{2,6},{3,7},{4,0},{5,1},{6,2},{7,3},{8,12},{9,13},{10,... | collective-permute-start | bytes 1572872 | tf_op jit(solution)/shard_map/ppermute | solution.py:12
  259.8 22.3 %collective-permute-start.15 = (f32[8,128,128]{2,1,0:T(8,128)}, f32[8,128,128]{2,1,0:T(8,128)S(1)}, u32[]{:S(2)}, u32[]{:S(2)}) collective-permute-start(f32[8,128,128]{2,1,0:T(8,128)} %dynamic-slice_select_fusion), channel_id=1, source_target_pairs={{0,8},{1,9},{2,10},{3,11},{4,12},{5,13},{6,14},{7,15},{8,0},{9,1},... | collective-permute-start | bytes 1572872 | tf_op jit(solution)/shard_map/ppermute | solution.py:12
  284.2 8.4 %collective-permute-start.17 = (f32[4,128,128]{2,1,0:T(8,128)S(1)}, f32[4,128,128]{2,1,0:T(8,128)S(1)}, u32[]{:S(2)}, u32[]{:S(2)}) collective-permute-start(f32[4,128,128]{2,1,0:T(8,128)S(1)} %dynamic-slice_select_fusion.9), channel_id=1, source_target_pairs={{0,2},{1,3},{2,0},{3,1},{4,6},{5,7},{6,4},{7,5},{8,10},{9,11},{10,... | collective-permute-start | bytes 786440 | tf_op jit(solution)/shard_map/ppermute | solution.py:12
  292.8 7.6 %collective-permute-start.18 = (f32[4,128,128]{2,1,0:T(8,128)S(1)}, f32[4,128,128]{2,1,0:T(8,128)S(1)}, u32[]{:S(2)}, u32[]{:S(2)}) collective-permute-start(f32[4,128,128]{2,1,0:T(8,128)S(1)} %dynamic-slice_select_fusion.8), channel_id=1, source_target_pairs={{0,4},{1,5},{2,6},{3,7},{4,0},{5,1},{6,2},{7,3},{8,12},{9,13},{10,... | collective-permute-start | bytes 786440 | tf_op jit(solution)/shard_map/ppermute | solution.py:12
  300.6 13.2 %collective-permute-start.19 = (f32[4,128,128]{2,1,0:T(8,128)S(1)}, f32[4,128,128]{2,1,0:T(8,128)S(1)}, u32[]{:S(2)}, u32[]{:S(2)}) collective-permute-start(f32[4,128,128]{2,1,0:T(8,128)S(1)} %dynamic-slice_select_fusion.7), channel_id=1, source_target_pairs={{0,8},{1,9},{2,10},{3,11},{4,12},{5,13},{6,14},{7,15},{8,0},{9,1},... | collective-permute-start | bytes 786440 | tf_op jit(solution)/shard_map/ppermute | solution.py:12
  315.8 8.4 %collective-permute-start.21 = (f32[4,128,128]{2,1,0:T(8,128)S(1)}, f32[4,128,128]{2,1,0:T(8,128)S(1)}, u32[]{:S(2)}, u32[]{:S(2)}) collective-permute-start(f32[4,128,128]{2,1,0:T(8,128)S(1)} %dynamic-slice_select_fusion.5), channel_id=1, source_target_pairs={{0,2},{1,3},{2,0},{3,1},{4,6},{5,7},{6,4},{7,5},{8,10},{9,11},{10,... | collective-permute-start | bytes 786440 | tf_op jit(solution)/shard_map/ppermute | solution.py:12
  324.4 7.6 %collective-permute-start.22 = (f32[4,128,128]{2,1,0:T(8,128)S(1)}, f32[4,128,128]{2,1,0:T(8,128)S(1)}, u32[]{:S(2)}, u32[]{:S(2)}) collective-permute-start(f32[4,128,128]{2,1,0:T(8,128)S(1)} %dynamic-slice_select_fusion.4), channel_id=1, source_target_pairs={{0,4},{1,5},{2,6},{3,7},{4,0},{5,1},{6,2},{7,3},{8,12},{9,13},{10,... | collective-permute-start | bytes 786440 | tf_op jit(solution)/shard_map/ppermute | solution.py:12
  332.1 13.2 %collective-permute-start.23 = (f32[4,128,128]{2,1,0:T(8,128)S(1)}, f32[4,128,128]{2,1,0:T(8,128)S(1)}, u32[]{:S(2)}, u32[]{:S(2)}) collective-permute-start(f32[4,128,128]{2,1,0:T(8,128)S(1)} %dynamic-slice_select_fusion.3), channel_id=1, source_target_pairs={{0,8},{1,9},{2,10},{3,11},{4,12},{5,13},{6,14},{7,15},{8,0},{9,1},... | collective-permute-start | bytes 786440 | tf_op jit(solution)/shard_map/ppermute | solution.py:12
  (17 other events, 218.4 us)
where the time goes:
time: 351 us; the launch traced here: 350 us
  waiting for transfers between devices  173 us (49%)
  blocking collectives  65.3 us (19%)
  starting transfers between devices  40.3 us (11%)
  other arithmetic  34.4 us (10%)
  local copies, waits for them, and re-layouts  19.1 us (5%)
  between operations  18 us (5%)
    ppermute x60, waiting for transfers between devices, swapped(): return lax.ppermute(value, axis, pairs)  173 us
    ppermute x60, starting transfers between devices, swapped(): return lax.ppermute(value, axis, pairs)  40.3 us
    pmax x1, blocking collectives, shards(): peak_loads.append(lax.pmax(holding.astype(jnp.float32), 'cube'))  33.7 us
    psum x1, blocking collectives, shards(): total_load = lax.psum(jnp.sum(initial_load.astype(jnp.float32)), 'cube')  31.5 us
    dynamic_update_slice x24, other arithmetic, place_rows(): lax.dynamic_update_slice_in_dim(padded, landed, first_free, 0)[:slot_count]  9.93 us
    lt x12, other arithmetic, place_rows(): extra_index < incoming  7.59 us
  transfers between devices with their start and end apart: 60, of which 46 were waited for; matrix products, arithmetic and copies ran while one was open for 13% of the time, Pallas kernels for 0%

commit v1 on v0

v1 whole, which is shorter than its diff:
```python
import functools

import jax
import jax.numpy as jnp
from jax import lax
from jax.experimental import pallas as pl
from jax.experimental.pallas import tpu as pltpu
from jax.sharding import PartitionSpec as P

SWEEPS = 3
CUBE = "cube"
GROUPS = "groups"


def capacity_classes(dims, slots):
    full = [slots * 2 ** min(b, dims - 1 - b) for b in range(dims)]
    plans = []
    for first, rest in ((8, 4), (10, 6), (12, 8), (16, 12)):
        plans.append(tuple(min(f, first if b == 0 else rest) for b, f in enumerate(full)))
    plans.append(tuple(full))
    return plans


def partner_rows(value, bit, index):
    size = value.shape[0]
    up = pltpu.roll(value, 2**bit, axis=0)
    down = pltpu.roll(value, size - 2**bit, axis=0)
    return jnp.where(((index >> bit) & 1) == 1, up, down)


def track(meta, cube, dims, slots):
    records = cube * slots
    wide = (cube, 128)
    row = lax.broadcasted_iota(jnp.int32, wide, 0)
    device = lax.broadcasted_iota(jnp.int32, (cube, records), 0)
    index = lax.broadcasted_iota(jnp.int32, (1, records), 1)
    origin, start = index // slots, index % slots
    load = jnp.broadcast_to(meta[:, 0:1], wide)

    def look_up(where, column):
        picked = jnp.where(device == where, jnp.broadcast_to(column[:, 0:1], device.shape), 0)
        return jnp.sum(picked, axis=0, keepdims=True)

    occupied = start < look_up(origin, load)
    at, pos = origin, start
    peaks = []
    for sweep in range(SWEEPS):
        for bit in range(dims):
            column = 1 + sweep * dims + bit
            count = jnp.broadcast_to(meta[:, column : column + 1], wide)
            free = load - count
            shift = partner_rows(free, bit, row) - free
            moves = occupied & (pos >= look_up(at, free))
            pos = pos + jnp.where(moves, look_up(at, shift), 0)
            at = jnp.where(moves, at ^ (2**bit), at)
            load = free + partner_rows(count, bit, row)
        peaks.append(jnp.max(load))
    total = jnp.sum(meta[:, 0:1].astype(jnp.float32))
    crossing = []
    for bit in range(dims):
        low = 2**bit - 1
        current = (at & low) | (origin & ~low)
        mover = occupied & ((((origin ^ at) >> bit) & 1) == 1)
        current = jnp.where(mover, current, -1)
        crossing.append((current, (device == current).astype(jnp.float32)))
    needs = [jnp.max(jnp.sum(hot, axis=1, keepdims=True)).astype(jnp.int32) for _, hot in crossing]
    return occupied, at, pos, load, start, peaks, total, crossing, needs


def plan_kernel(groups, cube, dims, slots, plans, width, meta_ref, ids_ref, tab_ref, word_ref, ids_out_ref, imb_ref):
    me, group = lax.axis_index(CUBE), lax.axis_index(GROUPS)
    records = cube * slots
    meta = meta_ref[pl.ds(pl.multiple_of(group * cube, cube), cube), :]
    occupied, at, pos, load, start, peaks, total, crossing, needs = track(meta, cube, dims, slots)
    for other in range(1, groups):
        there = lax.rem(group + other, groups)
        block = meta_ref[pl.ds(pl.multiple_of(there * cube, cube), cube), :]
        more = track(block, cube, dims, slots)[-1]
        needs = [jnp.maximum(a, b) for a, b in zip(needs, more)]
    choice = jnp.int32(len(plans) - 1)
    for k in reversed(range(len(plans) - 1)):
        fits = needs[0] <= plans[k][0]
        for b in range(1, dims):
            fits = fits & (needs[b] <= plans[k][b])
        choice = jnp.where(fits, k, choice)
    bases = []
    for b in range(dims):
        base = jnp.int32(0)
        for k, plan in enumerate(plans):
            base = jnp.where(choice == k, slots + sum(plan[:b]), base)
        bases.append(base)

    hot = jnp.concatenate([h for _, h in crossing], axis=0).astype(jnp.bfloat16)
    before = lax.broadcasted_iota(jnp.int32, (records, records), 0) < lax.broadcasted_iota(
        jnp.int32, (records, records), 1
    )
    ranks = jnp.dot(hot, before.astype(jnp.bfloat16), preferred_element_type=jnp.float32)
    slot = start
    rows, keys = [], []
    column = lax.broadcasted_iota(jnp.int32, (width, records), 0)
    for b in range(dims):
        current, own = crossing[b]
        rank = jnp.sum(own * ranks[b * cube : (b + 1) * cube], axis=0, keepdims=True).astype(jnp.int32)
        rows.append(slot)
        keys.append((column == jnp.where(current == me, rank, -1)).astype(jnp.float32))
        slot = jnp.where(current >= 0, bases[b] + rank, slot)
    rows += [slot, ids_ref[pl.ds(group, 1), :]]
    column = lax.broadcasted_iota(jnp.int32, (128, records), 0)
    keys.append((column == jnp.where(occupied & (at == me), pos, -1)).astype(jnp.float32))
    rows += [jnp.zeros((1, records), jnp.int32)] * (8 - len(rows))
    left = jnp.concatenate(rows, axis=0).astype(jnp.float32)
    right = jnp.concatenate(keys, axis=0)
    table = lax.dot_general(
        left, right, (((1,), (1,)), ((), ())),
        precision=lax.Precision.HIGHEST, preferred_element_type=jnp.float32,
    ).astype(jnp.int32)
    tab_ref[...] = table
    mine = lax.broadcasted_iota(jnp.int32, load.shape, 0) == me
    held = jnp.sum(jnp.where(mine, load, 0), axis=0, keepdims=True)
    lane = lax.broadcasted_iota(jnp.int32, (1, 128), 1)
    ids_out_ref[...] = jnp.where(lane < held, table[dims + 1 : dims + 2, dims * width : dims * width + 128], -1)
    word_ref[0] = choice
    word_ref[1] = jnp.max(held)
    peak = jnp.zeros((1, 128), jnp.float32)
    for sweep in range(SWEEPS):
        peak = jnp.where(lane == sweep, peaks[sweep].astype(jnp.float32), peak)
    imb_ref[...] = peak * float(cube) / total


def move_kernel(caps, slots, width, tab_ref, word_ref, adv_ref, out_ref, main, *scratch):
    dims = len(caps)
    outbox, recvs = scratch[0], scratch[1 : 1 + dims]
    send_sem, recv_sem, load_sem = scratch[1 + dims :]
    me = lax.axis_index(CUBE)
    partners = [me + 2**b - 2 * 2**b * ((me // 2**b) % 2) for b in range(dims)]
    fetch = pltpu.make_async_copy(adv_ref, main.at[pl.ds(0, slots)], load_sem)
    fetch.start()
    barrier = pltpu.get_barrier_semaphore()
    for p in partners:
        pl.semaphore_signal(barrier, inc=1, device_id={CUBE: p}, device_id_type=pl.DeviceIdType.MESH)
    pl.semaphore_wait(barrier, dims)
    fetch.wait()
    base = slots
    for b in range(dims):
        send, recv = outbox.at[pl.ds(0, caps[b])], recvs[b]

        def pack(j, carry):
            send[j] = main[tab_ref[b, b * width + j]]
            return carry

        lax.fori_loop(0, caps[b], pack, 0)
        copy = pltpu.make_async_remote_copy(
            src_ref=send, dst_ref=recv, send_sem=send_sem.at[b], recv_sem=recv_sem.at[b],
            device_id={CUBE: partners[b]}, device_id_type=pl.DeviceIdType.MESH,
        )
        copy.start()
        copy.wait()

        def keep(j, carry):
            main[base + j] = recv[j]
            return carry

        lax.fori_loop(0, caps[b], keep, 0)
        base += caps[b]

    held = word_ref[1]

    def place(j, carry):
        out_ref[j] = jnp.where(j < held, main[tab_ref[dims, dims * width + j]], 0.0)
        return carry

    lax.fori_loop(0, slots, place, 0)


def advect(field, ghost_rows, courant):
    western = jnp.concatenate([ghost_rows[:, 1, :][:, :, None], field[:, :, :-1]], 2)
    northern = jnp.concatenate([ghost_rows[:, 0, :][:, None, :], field[:, :-1, :]], 1)
    along_x = courant[:, 0][:, None, None]
    along_y = courant[:, 1][:, None, None]
    return field - along_x * (field - western) - along_y * (field - northern)


def shards(patches, ghost_rows, courant, patch_ids, initial_load, flow_counts):
    cube, groups = lax.axis_size(CUBE), lax.axis_size(GROUPS)
    dims = cube.bit_length() - 1
    slots, side = patches.shape[0], patches.shape[1]
    records = cube * slots
    plans = capacity_classes(dims, slots)
    width = max(plans[-1])
    tab_width = dims * width + 128

    mine = jnp.concatenate([initial_load, flow_counts[:, 0, :].reshape(-1)])
    mine = jnp.pad(mine, (0, 128 - slots - mine.shape[0]))
    mine = jnp.concatenate([mine, patch_ids])
    everyone = lax.all_gather(mine, (GROUPS, CUBE))
    ids = everyone[:, 128 - slots :].reshape(groups, records)

    vmem, smem = pl.BlockSpec(memory_space=pltpu.VMEM), pl.BlockSpec(memory_space=pltpu.SMEM)
    tab, word, final_ids, imbalance = pl.pallas_call(
        functools.partial(plan_kernel, groups, cube, dims, slots, plans, width),
        out_shape=(
            jax.ShapeDtypeStruct((8, tab_width), jnp.int32),
            jax.ShapeDtypeStruct((8,), jnp.int32),
            jax.ShapeDtypeStruct((1, 128), jnp.int32),
            jax.ShapeDtypeStruct((1, 128), jnp.float32),
        ),
        in_specs=[vmem, vmem],
        out_specs=(vmem, smem, vmem, vmem),
    )(everyone, ids)
    advected = advect(patches, ghost_rows, courant)

    def mover(k):
        caps = plans[k]
        block = lambda n: pltpu.VMEM((n, side, side), jnp.float32)
        return pl.pallas_call(
            functools.partial(move_kernel, caps, slots, width),
            out_shape=jax.ShapeDtypeStruct((slots, side, side), jnp.float32),
            in_specs=[smem, smem, pl.BlockSpec(memory_space=pl.ANY)],
            out_specs=vmem,
            scratch_shapes=[block(slots + sum(caps))]
            + [block(max(caps))] + [block(n) for n in caps]
            + [pltpu.SemaphoreType.DMA((dims,)), pltpu.SemaphoreType.DMA((dims,)), pltpu.SemaphoreType.DMA],
            compiler_params=pltpu.CompilerParams(
                collective_id=k, has_side_effects=True, vmem_limit_bytes=62 * 2**20
            ),
        )

    placed = lax.switch(word[0], [mover(k) for k in range(len(plans))], tab, word, advected)
    return placed, final_ids[0, :slots], imbalance[0, :SWEEPS]


def solution(mesh):
    in_specs = (
        P((GROUPS, CUBE), None, None),
        P((GROUPS, CUBE), None, None),
        P((GROUPS, CUBE), None),
        P((GROUPS, CUBE)),
        P((GROUPS, CUBE)),
        P(None, (GROUPS, CUBE), None),
    )
    out_specs = (P((GROUPS, CUBE), None, None), P((GROUPS, CUBE)), P(GROUPS))
    return jax.shard_map(shards, mesh=mesh, in_specs=in_specs, out_specs=out_specs, check_vma=False)
```

time: 351 us -> 117 us (0.33)
  waiting for transfers between devices: 173 us -> 0 us
  Pallas kernels: 0 us -> 56.9 us
  starting transfers between devices: 40.3 us -> 0 us
  other arithmetic: 34.4 us -> 5.5 us
  blocking collectives: 65.3 us -> 43.3 us
  between operations: 18 us -> 1.5 us
  local copies, waits for them, and re-layouts: 19.1 us -> 9.84 us
    ppermute x60 -> x0, waiting for transfers between devices: 173 us -> none  [swapped(): return lax.ppermute(value, axis, pairs)]
    pallas_call x0 -> x2, Pallas kernels: none -> 56.9 us  [the longest x1 54 us: shards(): lax.switch(word[0], [mover(k) for k in range(len(plans))], tab, word, adv...]
    all_gather x0 -> x1, blocking collectives: none -> 43.3 us  [shards(): everyone = lax.all_gather(mine, (GROUPS, CUBE))]
    ppermute x60 -> x0, starting transfers between devices: 40.3 us -> none  [swapped(): return lax.ppermute(value, axis, pairs)]
    pmax x1 -> x0, blocking collectives: 33.7 us -> none  [shards(): peak_loads.append(lax.pmax(holding.astype(jnp.float32), 'cube'))]
    psum x1 -> x0, blocking collectives: 31.5 us -> none  [shards(): total_load = lax.psum(jnp.sum(initial_load.astype(jnp.float32)), 'cube')]
    select_n x73 -> x0, other arithmetic: 10.1 us -> none  [the longest x47 6.02 us: place_rows(): retained = jnp.where(row_index < first_free, source, jnp.zeros_like(source))]
    dynamic_update_slice x24 -> x0, other arithmetic: 9.93 us -> none  [place_rows(): lax.dynamic_update_slice_in_dim(padded, landed, first_free, 0)[:slot_count]]
  transfers between devices with their start and end apart: 60 -> 0, of which waited for: 46 -> 0; matrix products, arithmetic and copies ran while one was open for 13% -> 0% of each run, Pallas kernels for 0% -> 0%
where the time goes in v1:
time: 117 us
  Pallas kernels  56.9 us (49%)
  blocking collectives  43.3 us (37%)
  local copies, waits for them, and re-layouts  9.84 us (8%)
  other arithmetic  5.5 us (5%)
  between operations  1.5 us (1%)
    pallas_call x1, Pallas kernels, shards(): lax.switch(word[0], [mover(k) for k in range(len(plans))], tab, word, adv...  54 us
    all_gather x1, blocking collectives, shards(): everyone = lax.all_gather(mine, (GROUPS, CUBE))  43.3 us
    sub x1, other arithmetic, advect(): return field - along_x * (field - western) - along_y * (field - northern)  4 us
    unnamed x5, local copies, waits for them, and re-layouts  3.14 us
    pallas_call x1, Pallas kernels, shards(): pl.pallas_call(functools.partial(plan_kernel, groups, cube, dims, slots,...  2.83 us

profile of v1, /device:TPU:0, one launch (start us, length us, event | category | flops | bytes accessed | tf_op | source)
XLA Modules:
  0.0 117.0 jit_solution(17941025437650006443)
XLA Ops:
  0.6 0.0 copy-start
  1.4 0.8 slice_bitcast_fusion.3
  2.2 0.7 reduce
  2.9 0.1 reshape_squeeze.3
  3.0 0.1 pad_add_fusion.1
  3.1 0.7 fusion.4
  3.8 43.3 %all-gather.1 = s32[32,1,128]{2,1,0:T(1,128)S(1)} all-gather(s32[1,1,128]{2,1,0:T(1,128)S(1)} %fusion.4), channel_id=2, replica_groups=mesh['groups'=2,'cube'=16] {'groups','cube'}, dimensions={0}, use_global_device_ids=true | all-gather | bytes 16896 | tf_op jit(solution)/shard_map/all_gather | solution.py:195
  47.1 0.0 copy-start.1
  47.1 0.1 slice.40
  47.1 0.7 reshape.14.ids_ref
  47.8 0.0 copy-done.1
  47.8 2.8 %shard_map.85 = (s32[8,384]{1,0:T(8,128)S(1)}, s32[8]{0:T(128)S(1)}, s32[1,128]{1,0:T(1,128)}, f32[1,128]{1,0:T(1,128)}) custom-call(s32[32,128]{1,0:T(8,128)} %bitcast.21, s32[2,512]{1,0:T(2,128)} %reshape.14.ids_ref), custom_call_target="tpu_custom_call" | custom-call | tf_op jit(solution)/shard_map/pallas_call | solution.py:199
  50.7 1.2 slice_bitcast_fusion.1
  51.8 1.1 slice_bitcast_fusion
  53.0 0.9 fusion.5
  53.8 2.0 %copy.15 = f32[32,128,1]{2,1,0:T(8,128)} copy(f32[32,128,1]{1,0,2:T(8,128)S(1)} %bitcast.22) | data formatting | bytes 32768 | tf_op jit(solution)/shard_map/broadcast_in_dim;squeeze | solution.py:176
  55.8 0.0 copy-done
  55.8 4.0 %fusion.2 = f32[32,128,128]{2,1,0:T(8,128)} fusion(f32[32,128,128]{2,1,0:T(8,128)S(1)} %copy-done, f32[32,128,127]{2,1,0:T(8,128)S(1)} %bitcast.18, f32[32,128,1]{2,1,0:T(8,128)} %copy.15, f32[32,127,128]{2,1,0:T(8,128)S(1)} %bitcast.19, f32[32,1,128]{2,1,0:T(1,128)S(1)} %get-tuple-element.62, f32[32]{0:T(128)S(1)} %get-tuple-element.65, ...), kind=kLoop, calls=%fused_computation.3 | loop fusion | flops 4194304 | bytes 8388864 | tf_op jit(solution)/shard_map/sub | solution.py:180
  59.8 54.0 %conditional.1 = (f32[32,128,128]{2,1,0:T(8,128)}) conditional(s32[]{:T(128)} %bitcast.2, (s32[8,384]{1,0:T(8,128)S(1)}, s32[8]{0:T(128)S(1)}, f32[32,128,128]{2,1,0:T(8,128)}) %tuple.23, (s32[8,384]{1,0:T(8,128)S(1)}, s32[8]{0:T(128)S(1)}, f32[32,128,128]{2,1,0:T(8,128)}) %tuple.23, (s32[8,384]{1,0:T(8,128)S(1)}, ...), branch_computations={%region_0.1_spmd, %region_1.2_spmd, %region_2.3_spmd, %region_3.4_... | conditional | bytes 8 | solution.py:228
  59.8 54.0 %branch_2_fun.1 = f32[32,128,128]{2,1,0:T(8,128)} custom-call(s32[8,384]{1,0:T(8,128)S(1)} %get-tuple-element.42.tab_ref, s32[8]{0:T(128)S(1)} %get-tuple-element.43.word_ref, f32[32,128,128]{2,1,0:T(8,128)} %get-tuple-element.44.adv_ref), custom_call_target="tpu_custom_call" | custom-call | tf_op jit(solution)/shard_map/cond/branch_2_fun/pallas_call | solution.py:228
  113.8 3.1 %copy.24 = f32[32,128,128]{2,1,0:T(8,128)} copy(f32[32,128,128]{2,1,0:T(8,128)} %get-tuple-element.72) | data formatting | bytes 4194304
Async XLA Ops:
  0.6 55.2 %copy-start = (f32[32,128,128]{2,1,0:T(8,128)S(1)}, f32[32,128,128]{2,1,0:T(8,128)}, u32[]{:S(2)}) copy-start(f32[32,128,128]{2,1,0:T(8,128)} %param.11) | copy-start | bytes 6291460
  47.1 0.8 copy-start.1
